TPU v7x, 32 devices: a whole 2x2x4 slice. The times are simulated.
32 devices in a mesh: gx: 4 (over z), gy: 4 (over y, core), gz: 2 (over x).
Axes of the slice: x: 2, y: 2, z: 4, core: 2. Of those that a mesh axis runs over, the one named last changes fastest.
Arguments:
- right_side: float32 [128, 128, 256], P('gx', 'gy', 'gz'), may hold values from -8 to 8
- guess: float32 [128, 128, 256], P('gx', 'gy', 'gz'), may hold values from -4 to 4
Outputs:
- solution_field: float32 [128, 128, 256], P('gx', 'gy', 'gz')
- residual: float32 [128, 128, 256], P('gx', 'gy', 'gz')
All inputs are finite; a program needn't handle non-finite values.
Results may differ from a plain program's by a relative error of at most 0.0001.
Values sent between devices are 32-bit elements; how exact they have to be, the bound alone decides.
A program may use at most 128 MiB of HBM per device.

v0:
```python
import jax
import jax.numpy as jnp
from jax import lax
from jax.sharding import PartitionSpec as P

LEVELS = 6
SWEEPS = 4
STEPS = 2


damping = 2.0 / 3.0


def passed_along(value, axis, steps):
    count = lax.axis_size(axis)
    first, last = (max(0, -steps), min(count, count - steps))
    return lax.ppermute(value, axis, [(source, source + steps) for source in range(first, last)])


def padded_2(x, sides, width):
    for axis, dim in sides:
        count, length = (lax.axis_size(axis), x.shape[dim])
        up = [(i, (i + 1) % count) for i in range(count - 1)]
        down = [(j, i) for i, j in up]
        last = lax.slice_in_dim(x, length - width, length, axis=dim)
        first = lax.slice_in_dim(x, 0, width, axis=dim)
        before = lax.ppermute(last, axis, up)
        after = lax.ppermute(first, axis, down)
        x = jnp.concatenate([before, x, after], axis=dim)
    return x


def padded_stencil(padded):
    beside = padded[2:, 1:-1, 1:-1] + padded[:-2, 1:-1, 1:-1]
    beside = beside + padded[1:-1, 2:, 1:-1] + padded[1:-1, :-2, 1:-1]
    beside = beside + padded[1:-1, 1:-1, 2:] + padded[1:-1, 1:-1, :-2]
    return 6.0 * padded[1:-1, 1:-1, 1:-1] - beside


def restrict(field):
    first, second, third = field.shape
    blocks = field.reshape(first // 2, 2, second // 2, 2, third // 2, 2)
    return jnp.mean(blocks, axis=(1, 3, 5))


def prolong(field):
    first, second, third = field.shape
    spread = jnp.broadcast_to(field[:, None, :, None, :, None], (first, 2, second, 2, third, 2))
    return spread.reshape(first * 2, second * 2, third * 2)


def axis_layers(packed, axis_name, by):
    if axis_name == "gx":
        return passed_along(packed, "gx", by)
    if axis_name == "gy":
        return passed_along(packed, "gy", by)
    return passed_along(packed, "gz", by)


def extend_all(fields, margin):
    current = list(fields)
    for dim_index, axis_name in ((0, "gx"), (1, "gy"), (2, "gz")):
        lows = [lax.slice_in_dim(f, 0, margin, axis=dim_index) for f in current]
        highs = [
            lax.slice_in_dim(f, f.shape[dim_index] - margin, f.shape[dim_index], axis=dim_index)
            for f in current
        ]
        received = {}
        for by in (1, -1):
            pieces = highs if by == 1 else lows
            packed = jnp.concatenate([p.reshape(-1) for p in pieces])
            received[by] = axis_layers(packed, axis_name, by)
        grown = []
        offset = 0
        for index, field in enumerate(current):
            piece_shape = lows[index].shape
            count = lows[index].size
            from_lower = received[1][offset : offset + count].reshape(piece_shape)
            from_upper = received[-1][offset : offset + count].reshape(piece_shape)
            offset = offset + count
            grown.append(jnp.concatenate([from_lower, field, from_upper], axis=dim_index))
        current = grown
    return current


def smooth_merged(items):
    results = {}
    approxes = [damping * rhs / (6.0 * 0.25**lev) for rhs, lev in items]
    for sweep_index in range(SWEEPS - 1):
        padded_list = extend_all(approxes, 1)
        renewed = []
        for index, (rhs, lev) in enumerate(items):
            scaling = 0.25**lev
            diagonal_value = 6.0 * scaling
            renewed.append(
                approxes[index]
                + damping * (rhs - scaling * padded_stencil(padded_list[index])) / diagonal_value
            )
        approxes = renewed
    for index, (rhs, lev) in enumerate(items):
        results[lev] = approxes[index]
    return results


def precondition(residual):
    chain = [residual]
    for level_index in range(1, LEVELS):
        chain.append(restrict(chain[-1]))
    first_level = LEVELS - 1
    local_levels = list(range(first_level + 1))
    smoothed = smooth_merged([(chain[lev], lev) for lev in local_levels])
    correction = smoothed[first_level]
    for level_index in range(first_level - 1, -1, -1):
        correction = prolong(correction) + smoothed[level_index]
    return correction


def apply_fine(field):
    padded = padded_2(field, (("gx", 0), ("gy", 1), ("gz", 2)), 1)
    return padded_stencil(padded)


def shards(right_side, guess):
    solution_field = guess
    residual = right_side - apply_fine(guess)
    for step_index in range(STEPS):
        direction = precondition(residual)
        image = apply_fine(direction)
        along, curvature = lax.psum(
            (jnp.sum(residual * direction), jnp.sum(direction * image)), ("gx", "gy", "gz")
        )
        alpha = along / curvature
        solution_field = solution_field + alpha * direction
        residual = residual - alpha * image
    return (solution_field, residual)


def solution(mesh):
    placed = (P("gx", "gy", "gz"), P("gx", "gy", "gz"))
    return jax.shard_map(
        shards,
        mesh=mesh,
        in_specs=placed,
        out_specs=(P("gx", "gy", "gz"), P("gx", "gy", "gz")),
        check_vma=False,
    )
```

profile of v0, /device:TPU:0, one launch (start us, length us, event | category | flops | bytes accessed | tf_op | source)
XLA Modules:
  0.0 606.6 jit_solution(4249604036732145625)
XLA Ops:
  2.7 5.6 collective-permute-start.1
  11.0 3.0 collective-permute-start.3
  17.2 4.5 collective-permute-start.5
  25.7 34.9 %reshape.1638 = f32[16,2,16,2,64,2]{5,4,3,2,1,0:T(8,128)} reshape(f32[32,32,128]{2,1,0:T(8,128)S(1)} %copy.405) | data formatting | bytes 1048576 | tf_op jit(solution)/shard_map/reshape | solution.py:42
  60.5 12.2 %reduce_sum.140 = f32[16,16,64]{2,1,0:T(8,128)S(1)} reduce(f32[16,2,16,2,64,2]{5,4,3,2,1,0:T(8,128)} %reshape.1638, f32[]{:T(128)} %constant.169.clone.1), dimensions={1,3,5}, to_apply=%region_0.0 | reduce | flops 114688 | bytes 589828 | tf_op jit(solution)/shard_map/reduce_sum | solution.py:43
  72.8 5.6 div.223
  78.4 2.6 reduce_sum.141
  82.3 4.2 collective-permute-start.7
  88.3 4.3 collective-permute-done.6
  97.4 5.7 collective-permute-done.8
  109.0 4.7 collective-permute-start.11
  122.3 3.5 collective-permute-start.13
  128.3 4.4 collective-permute-done.12
  138.2 3.5 collective-permute-done.14
  147.7 4.5 collective-permute-start.17
  163.2 3.5 collective-permute-start.19
  170.4 4.4 collective-permute-done.18
  180.3 3.5 collective-permute-done.20
  190.2 4.9 collective-permute-start.23
  204.2 4.9 reshape.1846
  210.7 11.4 %broadcast_in_dim.39 = f32[16,2,16,2,64,2]{5,4,3,2,1,0:T(8,128)} broadcast(f32[16,16,64]{2,1,0:T(8,128)S(1)} %fusion.112), dimensions={0,2,4} | broadcast | bytes 589824 | tf_op jit(solution)/shard_map/broadcast_in_dim | solution.py:48
  222.0 24.1 %reshape.1849 = f32[32,32,128]{2,1,0:T(8,128)S(1)} reshape(f32[16,2,16,2,64,2]{5,4,3,2,1,0:T(8,128)} %broadcast_in_dim.39) | data formatting | bytes 1048576 | tf_op jit(solution)/shard_map/reshape | solution.py:49
  250.0 4.5 collective-permute-start.25
  257.3 3.0 collective-permute-start.27
  263.5 4.5 collective-permute-start.29
  271.1 45.0 %all-reduce.1 = (f32[]{:T(128)}, f32[]{:T(128)}) all-reduce(f32[]{:T(128)} %get-tuple-element.9, f32[]{:T(128)} %get-tuple-element.8), channel_id=1, replica_groups=mesh['gx'=4,'gy'=4,'gz'=2] {'gx','gy','gz'}, use_global_device_ids=true, to_apply=%region_7.0 | all-reduce | flops 2 | bytes 16 | tf_op jit(solution)/shard_map/psum | solution.py:129
  317.9 34.9 %reshape.1852 = f32[16,2,16,2,64,2]{5,4,3,2,1,0:T(8,128)} reshape(f32[32,32,128]{2,1,0:T(8,128)S(1)} %copy.511) | data formatting | bytes 1048576 | tf_op jit(solution)/shard_map/reshape | solution.py:42
  352.7 12.2 %reduce_sum.149 = f32[16,16,64]{2,1,0:T(8,128)S(1)} reduce(f32[16,2,16,2,64,2]{5,4,3,2,1,0:T(8,128)} %reshape.1852, f32[]{:T(128)} %constant.169.clone.1), dimensions={1,3,5}, to_apply=%region_10.0 | reduce | flops 114688 | bytes 589828 | tf_op jit(solution)/shard_map/reduce_sum | solution.py:43
  365.0 5.6 div.269
  370.6 2.6 reduce_sum.150
  378.1 4.3 collective-permute-done.30
  387.2 4.3 collective-permute-done.32
  399.4 4.5 collective-permute-start.35
  412.0 2.6 collective-permute-start.37
  416.4 4.3 collective-permute-done.36
  426.5 3.2 collective-permute-done.38
  437.6 4.5 collective-permute-start.41
  450.2 3.9 collective-permute-start.43
  455.9 4.4 collective-permute-done.42
  465.8 3.5 collective-permute-done.44
  477.2 4.8 collective-permute-start.47
  488.1 4.9 reshape.2060
  493.8 11.4 %broadcast_in_dim.87 = f32[16,2,16,2,64,2]{5,4,3,2,1,0:T(8,128)} broadcast(f32[16,16,64]{2,1,0:T(8,128)S(1)} %fusion.81), dimensions={0,2,4} | broadcast | bytes 589824 | tf_op jit(solution)/shard_map/broadcast_in_dim | solution.py:48
  505.1 24.5 %reshape.2063 = f32[32,32,128]{2,1,0:T(8,128)} reshape(f32[16,2,16,2,64,2]{5,4,3,2,1,0:T(8,128)} %broadcast_in_dim.87) | data formatting | bytes 1048576 | tf_op jit(solution)/shard_map/reshape | solution.py:49
  533.8 4.5 collective-permute-start.49
  541.1 3.0 collective-permute-start.51
  547.9 4.5 collective-permute-start.53
  556.4 44.8 %all-reduce = (f32[]{:T(128)}, f32[]{:T(128)}) all-reduce(f32[]{:T(128)} %get-tuple-element.7, f32[]{:T(128)} %get-tuple-element.6), channel_id=1, replica_groups=mesh['gx'=4,'gy'=4,'gz'=2] {'gx','gy','gz'}, use_global_device_ids=true, to_apply=%region_17.0 | all-reduce | flops 2 | bytes 16 | tf_op jit(solution)/shard_map/psum | solution.py:129
  (1024 shorter events, 185.8 us)
Async XLA Ops:
  1.4 8.2 %collective-permute-start = (f32[1,32,128]{2,0,1:T(1,128)S(1)}, f32[1,32,128]{2,0,1:T(1,128)S(1)}, u32[]{:S(2)}, u32[]{:S(2)}) collective-permute-start(f32[1,32,128]{2,0,1:T(1,128)S(1)} %bitcast.399), channel_id=1, source_target_pairs={{8,0},{16,8},{24,16},{9,1},{17,9},{25,17},{10,2},{18,10},{26,18},{... | collective-permute-start | bytes 49160 | tf_op jit(solution)/shard_map/ppermute | solution.py:28
  2.7 7.0 %collective-permute-start.1 = (f32[1,32,128]{2,0,1:T(1,128)S(1)}, f32[1,32,128]{2,0,1:T(1,128)S(1)}, u32[]{:S(2)}, u32[]{:S(2)}) collective-permute-start(f32[1,32,128]{2,0,1:T(1,128)S(1)} %bitcast.398), channel_id=1, source_target_pairs={{0,8},{8,16},{16,24},{1,9},{9,17},{17,25},{2,10},{10,18},{18,26},{... | collective-permute-start | bytes 49160 | tf_op jit(solution)/shard_map/ppermute | solution.py:27
  9.7 4.3 collective-permute-start.2
  11.0 3.9 collective-permute-start.3
  15.5 6.2 %collective-permute-start.4 = (f32[34,34,1]{1,2,0:T(1,128)S(1)}, f32[34,34,1]{1,2,0:T(1,128)S(1)}, u32[]{:S(2)}, u32[]{:S(2)}) collective-permute-start(f32[34,34,1]{1,2,0:T(1,128)S(1)} %copy.400), channel_id=1, source_target_pairs={{1,0},{3,2},{5,4},{7,6},{9,8},{11,10},{13,12},{15,14},{17,16},{19,... | collective-permute-start | bytes 13880 | tf_op jit(solution)/shard_map/ppermute | solution.py:28
  17.2 6.0 collective-permute-start.5
  82.3 5.9 collective-permute-start.7
  86.9 5.7 collective-permute-start.6
  95.9 7.1 %collective-permute-start.8 = (f32[5964]{0:T(1024)S(1)}, f32[5964]{0:T(1024)S(1)}, u32[]{:S(2)}, u32[]{:S(2)}) collective-permute-start(f32[5964]{0:T(1024)S(1)} %concatenate.1027), channel_id=1, source_target_pairs={{2,0},{4,2},{6,4},{3,1},{5,3},{7,5},{10,8},{12,10},{14,12},{11,9},... | collective-permute-start | bytes 71576 | tf_op jit(solution)/shard_map/ppermute | solution.py:17
  106.6 7.2 %collective-permute-start.10 = (f32[1641]{0:T(1024)S(1)}, f32[1641]{0:T(1024)S(1)}, u32[]{:S(2)}, u32[]{:S(2)}) collective-permute-start(f32[1641]{0:T(1024)S(1)} %concatenate.1035), channel_id=1, source_target_pairs={{1,0},{3,2},{5,4},{7,6},{9,8},{11,10},{13,12},{15,14},{17,16},{19,... | collective-permute-start | bytes 19700 | tf_op jit(solution)/shard_map/ppermute | solution.py:17
  109.0 5.9 collective-permute-start.11
  122.3 5.9 collective-permute-start.13
  126.9 5.8 collective-permute-start.12
  136.7 5.0 collective-permute-start.14
  145.3 7.0 %collective-permute-start.16 = (f32[1641]{0:T(1024)S(1)}, f32[1641]{0:T(1024)S(1)}, u32[]{:S(2)}, u32[]{:S(2)}) collective-permute-start(f32[1641]{0:T(1024)S(1)} %concatenate.1085), channel_id=1, source_target_pairs={{1,0},{3,2},{5,4},{7,6},{9,8},{11,10},{13,12},{15,14},{17,16},{19,... | collective-permute-start | bytes 19700 | tf_op jit(solution)/shard_map/ppermute | solution.py:17
  147.7 5.9 collective-permute-start.17
  163.2 7.2 %collective-permute-start.19 = (f32[5460]{0:T(1024)S(1)}, f32[5460]{0:T(1024)S(1)}, u32[]{:S(2)}, u32[]{:S(2)}) collective-permute-start(f32[5460]{0:T(1024)S(1)} %concatenate.1120), channel_id=1, source_target_pairs={{0,8},{8,16},{16,24},{1,9},{9,17},{17,25},{2,10},{10,18},{18,26},{... | collective-permute-start | bytes 65528 | tf_op jit(solution)/shard_map/ppermute | solution.py:17
  169.1 5.8 collective-permute-start.18
  178.8 5.0 collective-permute-start.20
  187.7 7.4 %collective-permute-start.22 = (f32[1641]{0:T(1024)S(1)}, f32[1641]{0:T(1024)S(1)}, u32[]{:S(2)}, u32[]{:S(2)}) collective-permute-start(f32[1641]{0:T(1024)S(1)} %concatenate.1135), channel_id=1, source_target_pairs={{1,0},{3,2},{5,4},{7,6},{9,8},{11,10},{13,12},{15,14},{17,16},{19,... | collective-permute-start | bytes 19700 | tf_op jit(solution)/shard_map/ppermute | solution.py:17
  190.2 5.9 collective-permute-start.23
  248.7 5.9 collective-permute-start.24
  250.0 6.0 collective-permute-start.25
  256.0 4.3 collective-permute-start.26
  257.3 3.9 collective-permute-start.27
  261.8 6.2 %collective-permute-start.28 = (f32[34,34,1]{1,2,0:T(1,128)S(1)}, f32[34,34,1]{1,2,0:T(1,128)S(1)}, u32[]{:S(2)}, u32[]{:S(2)}) collective-permute-start(f32[34,34,1]{1,2,0:T(1,128)S(1)} %copy.506), channel_id=1, source_target_pairs={{1,0},{3,2},{5,4},{7,6},{9,8},{11,10},{13,12},{15,14},{17,16},{19,... | collective-permute-start | bytes 13880 | tf_op jit(solution)/shard_map/ppermute | solution.py:28
  263.5 6.0 collective-permute-start.29
  376.8 5.7 collective-permute-start.30
  385.7 5.8 collective-permute-start.32
  397.0 7.0 %collective-permute-start.34 = (f32[1641]{0:T(1024)S(1)}, f32[1641]{0:T(1024)S(1)}, u32[]{:S(2)}, u32[]{:S(2)}) collective-permute-start(f32[1641]{0:T(1024)S(1)} %concatenate.1193), channel_id=1, source_target_pairs={{1,0},{3,2},{5,4},{7,6},{9,8},{11,10},{13,12},{15,14},{17,16},{19,... | collective-permute-start | bytes 19700 | tf_op jit(solution)/shard_map/ppermute | solution.py:17
  399.4 5.9 collective-permute-start.35
  412.0 4.3 collective-permute-start.37
  415.0 5.7 collective-permute-start.36
  422.3 4.1 collective-permute-start.39
  424.9 4.9 collective-permute-start.38
  435.2 7.0 %collective-permute-start.40 = (f32[1641]{0:T(1024)S(1)}, f32[1641]{0:T(1024)S(1)}, u32[]{:S(2)}, u32[]{:S(2)}) collective-permute-start(f32[1641]{0:T(1024)S(1)} %concatenate.1243), channel_id=1, source_target_pairs={{1,0},{3,2},{5,4},{7,6},{9,8},{11,10},{13,12},{15,14},{17,16},{19,... | collective-permute-start | bytes 19700 | tf_op jit(solution)/shard_map/ppermute | solution.py:17
  437.6 5.9 collective-permute-start.41
  450.2 5.6 collective-permute-start.43
  454.5 5.8 collective-permute-start.42
  464.3 5.0 collective-permute-start.44
  474.8 7.2 %collective-permute-start.46 = (f32[1641]{0:T(1024)S(1)}, f32[1641]{0:T(1024)S(1)}, u32[]{:S(2)}, u32[]{:S(2)}) collective-permute-start(f32[1641]{0:T(1024)S(1)} %concatenate.1293), channel_id=1, source_target_pairs={{1,0},{3,2},{5,4},{7,6},{9,8},{11,10},{13,12},{15,14},{17,16},{19,... | collective-permute-start | bytes 19700 | tf_op jit(solution)/shard_map/ppermute | solution.py:17
  477.2 5.9 collective-permute-start.47
  532.5 5.9 collective-permute-start.48
  533.8 6.0 collective-permute-start.49
  539.8 4.3 collective-permute-start.50
  541.1 3.9 collective-permute-start.51
  546.2 6.2 %collective-permute-start.52 = (f32[34,34,1]{1,2,0:T(1,128)S(1)}, f32[34,34,1]{1,2,0:T(1,128)S(1)}, u32[]{:S(2)}, u32[]{:S(2)}) collective-permute-start(f32[34,34,1]{1,2,0:T(1,128)S(1)} %copy.612), channel_id=1, source_target_pairs={{1,0},{3,2},{5,4},{7,6},{9,8},{11,10},{13,12},{15,14},{17,16},{19,... | collective-permute-start | bytes 13880 | tf_op jit(solution)/shard_map/ppermute | solution.py:28
  547.9 6.0 collective-permute-start.53
  (31 other events, 468.1 us)
where the time goes:
time: 617 us; the launch traced here: 607 us
  local copies, waits for them, and re-layouts  258 us (42%)
  starting transfers between devices  131 us (21%)
  blocking collectives  89.7 us (15%)
  waiting for transfers between devices  64.4 us (10%)
  other arithmetic  57.4 us (9%)
  between operations  6.56 us (1%)
    psum x2, blocking collectives, shards(): lax.psum((jnp.sum(residual * direction), jnp.sum(direction * image)), ('g...  89.7 us
    ppermute x36, starting transfers between devices, passed_along(): lax.ppermute(value, axis, [(source, source + steps) for source in range(f...  81.6 us
    reshape x2, local copies, waits for them, and re-layouts, restrict(): blocks = field.reshape(first // 2, 2, second // 2, 2, third // 2, 2)  69.7 us
    reshape x8, local copies, waits for them, and re-layouts, prolong(): return spread.reshape(first * 2, second * 2, third * 2)  58.9 us
    ppermute x36, waiting for transfers between devices, passed_along(): lax.ppermute(value, axis, [(source, source + steps) for source in range(f...  56 us
    ppermute x9, starting transfers between devices, padded_2(): before = lax.ppermute(last, axis, up)  37.4 us
    reduce_sum x12, other arithmetic, restrict(): return jnp.mean(blocks, axis=(1, 3, 5))  30.3 us
    broadcast_in_dim x12, local copies, waits for them, and re-layouts, prolong(): jnp.broadcast_to(field[:, None, :, None, :, None], (first, 2, second, 2,...  28.4 us
  transfers between devices with their start and end apart: 54, of which 27 were waited for; matrix products, arithmetic and copies ran while one was open for 3% of the time, Pallas kernels for 0%

commit v1 on v0

v1 whole, which is shorter than its diff:
```python
import functools

import jax
import jax.numpy as jnp
from jax import lax
from jax.experimental import pallas as pl
from jax.experimental.pallas import tpu as pltpu
from jax.sharding import PartitionSpec as P

LEVELS = 6
SWEEPS = 4
STEPS = 2
HALOED = 3
AXES = ("gx", "gy", "gz")
LANES = 128
TOP = 8
MESH = pl.DeviceIdType.MESH
ROUNDS = 1 + STEPS * SWEEPS
HIGH = lax.Precision.HIGHEST


def iota(shape, dim):
    return lax.broadcasted_iota(jnp.int32, shape, dim)


def lanes_dot(x, matrix):
    first, second, _ = x.shape
    if second % 8 == 0:
        out = jnp.dot(x.reshape(first * second, LANES), matrix, precision=HIGH, preferred_element_type=jnp.float32)
        return out.reshape(first, second, LANES)
    planes = [jnp.dot(x[i], matrix, precision=HIGH, preferred_element_type=jnp.float32)[None] for i in range(first)]
    return jnp.concatenate(planes, axis=0)


def halve_matrix(width, start):
    source, target = iota((LANES, LANES), 0), iota((LANES, LANES), 1) - start
    keep = (target >= 0) & (target < width) & ((source == 2 * target) | (source == 2 * target + 1))
    return jnp.where(keep, 0.125, 0.0)


def double_matrix(width, start):
    source, target = iota((LANES, LANES), 0) - start, iota((LANES, LANES), 1)
    keep = (source >= 0) & (source < width) & ((target == 2 * source) | (target == 2 * source + 1))
    return jnp.where(keep, 1.0, 0.0)


def kernel(sizes, block, b_ref, x_ref, sol_ref, res_ref, *rest):
    (u0a, u0b, u1a, u1b, u2a, u2b, g0, g1, g2, wref, fold, spread,
     xs, xr, ys, yr, zs, zr, gs, gr, ds, dr,
     hsend, hrecv, gsend, grecv, dsend, drecv) = rest
    us = ((u0a, u0b), (u1a, u1b), (u2a, u2b))
    gref = (g0, g1, g2)
    nx, ny, nz = sizes
    n = nx * ny * nz
    at = tuple(lax.axis_index(a) for a in AXES)
    me = (at[0] * ny + at[1]) * nz + at[2]
    dims = [tuple(d >> l for d in block) for l in range(LEVELS)]

    def place(index):
        return (index // (ny * nz), index // nz % ny, index % nz)

    xr[...] = jnp.zeros_like(xr)
    yr[...] = jnp.zeros_like(yr)
    zr[...] = jnp.zeros_like(zr)

    barrier = pltpu.get_barrier_semaphore()

    def greet(k, _):
        pl.semaphore_signal(barrier, inc=1, device_id=place((me + k) % n), device_id_type=MESH)
        return 0

    lax.fori_loop(1, n, greet, 0)
    pl.semaphore_wait(barrier, n - 1)

    row_off, lane_off = [0], [0]
    for l in range(HALOED):
        row_off.append(row_off[-1] + dims[l][0])
        lane_off.append(lane_off[-1] + 2 * dims[l][0])

    def halo_copies(r, levels):
        rows = row_off[levels]
        out = []
        for d, (s, t) in enumerate(((xs, xr), (ys, yr), (zs, zr))):
            for side in (0, 1):
                target = list(at)
                target[d] = at[d] + (1 if side else -1)
                src = s.at[r] if d == 2 else s.at[r, side, pl.ds(0, rows)]
                dst = t.at[r, side] if d == 2 else t.at[r, side, pl.ds(0, rows)]
                copy = pltpu.make_async_remote_copy(
                    src_ref=src, dst_ref=dst,
                    send_sem=hsend.at[r, 2 * d + side], recv_sem=hrecv.at[r, 2 * d + side],
                    device_id=tuple(target), device_id_type=MESH,
                )
                lower, upper = at[d] > 0, at[d] < sizes[d] - 1
                out.append((copy, upper if side else lower, lower if side else upper))
        return out

    def send(r, fields, levels):
        for l in range(levels):
            X, Y, Z = dims[l]
            u = fields[l]
            o = row_off[l]
            for side, i in ((0, 1), (1, X)):
                xs[r, side, o:o + Y, :] = u[i, TOP:TOP + Y, :]
            for side, j in ((0, TOP), (1, TOP + Y - 1)):
                ys[r, side, o:o + X, :, :] = u[1:X + 1, j:j + 1, :]
            body = u[1:X + 1, TOP:TOP + Y, :]
            lane, plane = iota((X, Y, LANES), 2) - lane_off[l], iota((X, Y, LANES), 0)
            packed = jnp.where(lane == plane, body[:, :, Z - 1:Z], jnp.where(lane == plane + X, body[:, :, 0:1], 0.0))
            packed = jnp.sum(packed, axis=0)
            zs[r, 0:Y, :] = packed if l == 0 else zs[r, 0:Y, :] + packed
        for copy, cond, _ in halo_copies(r, levels):
            pl.when(cond)(copy.start)

    def receive(r, fields, levels):
        for copy, _, cond in halo_copies(r, levels):
            pl.when(cond)(copy.wait_recv)
        for l in range(levels):
            X, Y, Z = dims[l]
            u = fields[l]
            o = row_off[l]
            u[0, TOP:TOP + Y, :] = xr[r, 1, o:o + Y, :]
            u[X + 1, TOP:TOP + Y, :] = xr[r, 0, o:o + Y, :]
            u[1:X + 1, TOP - 1:TOP, :] = yr[r, 1, o:o + X, :, :]
            u[1:X + 1, TOP + Y:TOP + Y + 1, :] = yr[r, 0, o:o + X, :, :]

    def beside(r, u, l, x0, c):
        X, Y, Z = dims[l]
        mid = u[x0 + 1:x0 + 1 + c, TOP:TOP + Y, :]
        total = u[x0:x0 + c, TOP:TOP + Y, :] + u[x0 + 2:x0 + 2 + c, TOP:TOP + Y, :]
        total = total + u[x0 + 1:x0 + 1 + c, TOP - 1:TOP - 1 + Y, :]
        total = total + u[x0 + 1:x0 + 1 + c, TOP + 1:TOP + 1 + Y, :]
        lane = iota((c, Y, LANES), 2)
        o = lane_off[l] + x0
        low, high = zr[r, 1, 0:Y, :], zr[r, 0, 0:Y, :]
        below = jnp.concatenate([low[:, o + i:o + i + 1][None] for i in range(c)], axis=0)
        above = jnp.concatenate([high[:, o + X + i:o + X + i + 1][None] for i in range(c)], axis=0)
        total = total + jnp.where(lane == 0, below, pltpu.roll(mid, 1, 2))
        total = total + jnp.where(lane == Z - 1, above, pltpu.roll(mid, LANES - 1, 2))
        return mid, total

    def chunks(l):
        c = min(dims[l][0], 4)
        return [(x0, c) for x0 in range(0, dims[l][0], c)]

    def inside(l, x0, c):
        return (slice(x0 + 1, x0 + 1 + c), slice(TOP, TOP + dims[l][1]), slice(None))

    def fold_xy(field):
        X, Y, _ = field.shape
        pairs = field.reshape(X // 2, 2, Y, LANES)
        fold[0:X // 2, 0:Y, :] = pairs[:, 0] + pairs[:, 1]
        return fold[0:X // 2, pl.ds(0, Y // 2, 2), :] + fold[0:X // 2, pl.ds(1, Y // 2, 2), :]

    def spread_y(field):
        X, Y, _ = field.shape
        spread[0:X, pl.ds(0, Y, 2), :] = field
        spread[0:X, pl.ds(1, Y, 2), :] = field

    def twice(field):
        X, Y, _ = field.shape
        return jnp.broadcast_to(field[:, None], (X, 2, Y, LANES)).reshape(2 * X, Y, LANES)

    def all_copy(k, src, dst, s_sem, r_sem):
        return pltpu.make_async_remote_copy(
            src_ref=src, dst_ref=dst.at[me], send_sem=s_sem.at[k], recv_sem=r_sem.at[k],
            device_id=place((me + k) % n), device_id_type=MESH,
        )

    def to_all(step, src, dst, s_sem, r_sem, what):
        def one(k, _):
            copy = all_copy(k, src.at[step], dst.at[step], s_sem.at[step], r_sem.at[step])
            getattr(copy, what)()
            return 0
        lax.fori_loop(1, n, one, 0)

    X, Y, Z = dims[0]
    u0a[1:X + 1, TOP:TOP + Y, :] = x_ref[...]
    sol_ref[...] = x_ref[...]
    send(0, [u0a], 1)
    receive(0, [u0a], 1)
    for x0, c in chunks(0):
        mid, total = beside(0, u0a, 0, x0, c)
        g0[x0:x0 + c] = b_ref[x0:x0 + c] - (6.0 * mid - total)

    def smooth_whole(rhs, width, l):
        X, Y, _ = rhs.shape
        lane = iota(rhs.shape, 2)
        e = rhs
        for _ in range(SWEEPS - 1):
            px, py = jnp.zeros((1, Y, LANES), jnp.float32), jnp.zeros((X, 1, LANES), jnp.float32)
            total = jnp.concatenate([px, e[:-1]], axis=0) + jnp.concatenate([e[1:], px], axis=0)
            total = total + jnp.concatenate([py, e[:, :-1]], axis=1) + jnp.concatenate([e[:, 1:], py], axis=1)
            total = total + jnp.where(lane == 0, 0.0, pltpu.roll(e, 1, 2))
            total = total + jnp.where(lane == width - 1, 0.0, pltpu.roll(e, LANES - 1, 2))
            e = rhs + (3.0 * e + total) * (1.0 / 9.0)
        return e * (4.0 ** l / 9.0)

    for step in range(STEPS):
        base = 1 + step * SWEEPS
        for l in range(HALOED - 1):
            gref[l + 1][...] = lanes_dot(fold_xy(gref[l][...]), halve_matrix(dims[l + 1][2], 0))
        width = dims[HALOED][2]
        own = lanes_dot(fold_xy(gref[HALOED - 1][...]), halve_matrix(width, at[2] * width))
        gs[step] = own
        gr[step, me] = own
        to_all(step, gs, gr, gsend, grecv, "start")
        for l in range(HALOED):
            us[l][0][1:dims[l][0] + 1, TOP:TOP + dims[l][1], :] = gref[l][...]
        for sweep in range(SWEEPS - 1):
            r = base + sweep
            fields = [us[l][sweep % 2] for l in range(HALOED)]
            later = [us[l][(sweep + 1) % 2] for l in range(HALOED)]
            send(r, fields, HALOED)
            if sweep == SWEEPS - 2:
                to_all(step, gs, gr, gsend, grecv, "wait_recv")
                rows = []
                for i in range(nx):
                    columns = []
                    for j in range(ny):
                        part = gr[step, (i * ny + j) * nz]
                        for k in range(1, nz):
                            part = part + gr[step, (i * ny + j) * nz + k]
                        columns.append(part)
                    rows.append(jnp.concatenate(columns, axis=1))
                chain = [jnp.concatenate(rows, axis=0)]
                widths = [width * nz]
                for l in range(HALOED + 1, LEVELS):
                    widths.append(widths[-1] // 2)
                    chain.append(lanes_dot(fold_xy(chain[-1]), halve_matrix(widths[-1], 0)))
                whole = smooth_whole(chain[-1], widths[-1], LEVELS - 1)
                for l in range(LEVELS - 2, HALOED - 1, -1):
                    i = l - HALOED
                    spread_y(whole)
                    grown = spread[0:whole.shape[0], 0:2 * whole.shape[1], :]
                    grown = twice(lanes_dot(grown, double_matrix(widths[i + 1], 0)))
                    whole = grown + smooth_whole(chain[i], widths[i], l)
                wref[...] = whole
            receive(r, fields, HALOED)
            for l in range(HALOED):
                for x0, c in chunks(l):
                    mid, total = beside(r, fields[l], l, x0, c)
                    later[l][inside(l, x0, c)] = gref[l][x0:x0 + c] + (3.0 * mid + total) * (1.0 / 9.0)
        ends = [us[l][(SWEEPS - 1) % 2] for l in range(HALOED)]
        cx, cy, _ = dims[HALOED]
        spread_y(wref[pl.ds(at[0] * cx, cx)])
        part = spread[0:cx, pl.ds(pl.multiple_of(at[1] * 2 * cy, 8), 2 * cy), :]
        part = lanes_dot(part, double_matrix(width, at[2] * width))
        for l in range(HALOED - 1, -1, -1):
            X, Y, Z = dims[l]
            full = ends[l][1:X + 1, TOP:TOP + Y, :] * (4.0 ** l / 9.0) + twice(part)
            if l:
                spread_y(full)
                part = lanes_dot(spread[0:X, 0:2 * Y, :], double_matrix(Z, 0))
            else:
                ends[0][1:X + 1, TOP:TOP + Y, :] = full
        r = base + SWEEPS - 1
        z = ends[0]
        w = us[0][SWEEPS % 2]
        send(r, [z], 1)
        receive(r, [z], 1)
        rz = jnp.zeros((Y, LANES), jnp.float32)
        zw = jnp.zeros((Y, LANES), jnp.float32)
        for x0, c in chunks(0):
            mid, total = beside(r, z, 0, x0, c)
            image = 6.0 * mid - total
            w[inside(0, x0, c)] = image
            rz = rz + jnp.sum(g0[x0:x0 + c] * mid, axis=0)
            zw = zw + jnp.sum(mid * image, axis=0)
        sums = jnp.concatenate([jnp.sum(rz, axis=0, keepdims=True), jnp.sum(zw, axis=0, keepdims=True)], axis=0)
        ds[step] = sums
        dr[step, me] = sums
        to_all(step, ds, dr, dsend, drecv, "start")
        to_all(step, ds, dr, dsend, drecv, "wait_recv")
        both = jnp.sum(dr[step], axis=0)
        both = jnp.sum(both, axis=1, keepdims=True)
        alpha = (both[0:1] / both[1:2])[None]
        for x0, c in chunks(0):
            sol_ref[x0:x0 + c] = sol_ref[x0:x0 + c] + alpha * z[inside(0, x0, c)]
            renewed = g0[x0:x0 + c] - alpha * w[inside(0, x0, c)]
            if step == STEPS - 1:
                res_ref[x0:x0 + c] = renewed
            else:
                g0[x0:x0 + c] = renewed

    for step in range(STEPS):
        to_all(step, gs, gr, gsend, grecv, "wait_send")
        to_all(step, ds, dr, dsend, drecv, "wait_send")
    for r in range(ROUNDS):
        for copy, cond, _ in halo_copies(r, 1 if r % SWEEPS == 0 else HALOED):
            pl.when(cond)(copy.wait_send)


def solution(mesh):
    sizes = tuple(mesh.shape[a] for a in AXES)
    n = sizes[0] * sizes[1] * sizes[2]

    def run(right_side, guess):
        X, Y, Z = block = guess.shape
        dims = [tuple(d >> l for d in block) for l in range(LEVELS)]
        rows = sum(dims[l][0] for l in range(HALOED))
        f32 = jnp.float32
        vm = lambda *s: pltpu.VMEM(s, f32)
        padded = [vm(dims[l][0] + 2, dims[l][1] + 2 * TOP, LANES) for l in range(HALOED) for _ in range(2)]
        cx, cy, _ = dims[HALOED]
        scratch = padded + [vm(dims[l][0], dims[l][1], LANES) for l in range(HALOED)] + [
            vm(cx * sizes[0], cy * sizes[1], LANES),
            vm(X // 2, Y, LANES), vm(X // 2, Y, LANES),
            vm(ROUNDS, 2, rows, LANES), vm(ROUNDS, 2, rows, LANES),
            vm(ROUNDS, 2, rows, 1, LANES), vm(ROUNDS, 2, rows, 1, LANES),
            vm(ROUNDS, Y, LANES), vm(ROUNDS, 2, Y, LANES),
            vm(STEPS, cx, cy, LANES), vm(STEPS, n, cx, cy, LANES),
            vm(STEPS, 2, LANES), vm(STEPS, n, 2, LANES),
            pltpu.SemaphoreType.DMA((ROUNDS, 6)), pltpu.SemaphoreType.DMA((ROUNDS, 6)),
        ] + [pltpu.SemaphoreType.DMA((STEPS, n))] * 4
        out = jax.ShapeDtypeStruct(block, f32)
        return tuple(pl.pallas_call(
            functools.partial(kernel, sizes, block),
            out_shape=(out, out),
            in_specs=[pl.BlockSpec(memory_space=pltpu.VMEM)] * 2,
            out_specs=[pl.BlockSpec(memory_space=pltpu.VMEM)] * 2,
            scratch_shapes=scratch,
            compiler_params=pltpu.CompilerParams(collective_id=0, has_side_effects=True),
        )(right_side, guess))

    spec = P(*AXES)
    return jax.shard_map(run, mesh=mesh, in_specs=(spec, spec), out_specs=(spec, spec), check_vma=False)
```

time: 617 us -> 80.1 us (0.13); the launches traced: 607 us -> 79.9 us
  local copies, waits for them, and re-layouts: 258 us -> 2.72 us
  starting transfers between devices: 131 us -> 0 us
  blocking collectives: 89.7 us -> 0 us
  Pallas kernels: 0 us -> 76.6 us
  waiting for transfers between devices: 64.4 us -> 0 us
  other arithmetic: 57.4 us -> 0 us
    reshape x400 -> x0, local copies, waits for them, and re-layouts: 173 us -> none  [the longest x2 69.7 us: restrict(): blocks = field.reshape(first // 2, 2, second // 2, 2, third // 2, 2)]
    ppermute x54 -> x0, starting transfers between devices: 131 us -> none  [the longest x36 81.6 us: passed_along(): lax.ppermute(value, axis, [(source, source + steps) for source in range(f...]
    psum x2 -> x0, blocking collectives: 89.7 us -> none  [shards(): lax.psum((jnp.sum(residual * direction), jnp.sum(direction * image)), ('g...]
    pallas_call x0 -> x1, Pallas kernels: none -> 76.6 us  [run(): pl.pallas_call(functools.partial(kernel, sizes, block), out_shape=(out, o...]
    ppermute x54 -> x0, waiting for transfers between devices: 64.4 us -> none  [the longest x36 56 us: passed_along(): lax.ppermute(value, axis, [(source, source + steps) for source in range(f...]
    reduce_sum x14 -> x0, other arithmetic: 33.6 us -> none  [the longest x12 30.3 us: restrict(): return jnp.mean(blocks, axis=(1, 3, 5))]
    slice x288 -> x0, local copies, waits for them, and re-layouts: 31.9 us -> none  [the longest x48 14.8 us: extend_all(): lows = [lax.slice_in_dim(f, 0, margin, axis=dim_index) for f in current]]
    broadcast_in_dim x12 -> x0, local copies, waits for them, and re-layouts: 28.4 us -> none  [prolong(): jnp.broadcast_to(field[:, None, :, None, :, None], (first, 2, second, 2,...]
  transfers between devices with their start and end apart: 54 -> 0, of which waited for: 27 -> 0; matrix products, arithmetic and copies ran while one was open for 3% -> 0% of each run, Pallas kernels for 0% -> 0%
where the time goes in v1:
time: 80.1 us; the launch traced here: 79.9 us
  Pallas kernels  76.6 us (96%)
  local copies, waits for them, and re-layouts  2.72 us (3%)
    pallas_call x1, Pallas kernels, run(): pl.pallas_call(functools.partial(kernel, sizes, block), out_shape=(out, o...  76.6 us
    unnamed x4, local copies, waits for them, and re-layouts  2.72 us

profile of v1, /device:TPU:0, one launch (start us, length us, event | category | flops | bytes accessed | tf_op | source)
XLA Modules:
  0.0 79.9 jit_solution(9642097357931408874)
XLA Ops:
  0.6 76.6 %shard_map.41 = (f32[32,32,128]{2,1,0:T(8,128)}, f32[32,32,128]{2,1,0:T(8,128)}) custom-call(f32[32,32,128]{2,1,0:T(8,128)} %b_ref.1, f32[32,32,128]{2,1,0:T(8,128)} %x_ref.1), custom_call_target="tpu_custom_call" | custom-call | tf_op jit(solution)/shard_map/pallas_call | solution.py:317
  77.2 0.0 copy-start
  77.2 1.9 %copy.6 = f32[32,32,128]{2,1,0:T(8,128)} copy(f32[32,32,128]{2,1,0:T(8,128)} %get-tuple-element.4) | data formatting | bytes 1048576
  79.1 0.0 copy-done
  79.1 0.8 copy.7
Async XLA Ops:
  77.2 1.9 %copy-start = (f32[32,32,128]{2,1,0:T(8,128)S(1)}, f32[32,32,128]{2,1,0:T(8,128)}, u32[]{:S(2)}) copy-start(f32[32,32,128]{2,1,0:T(8,128)} %get-tuple-element.5) | copy-start | bytes 1572868

commit v2 on v1

--- a/solution.py
+++ b/solution.py
@@ -42,6 +42,25 @@
     source, target = iota((LANES, LANES), 0) - start, iota((LANES, LANES), 1)
     keep = (source >= 0) & (source < width) & ((target == 2 * source) | (target == 2 * source + 1))
     return jnp.where(keep, 1.0, 0.0)
+
+
+def plane_groups(shape, width):
+    return max(1, LANES // width // shape[1])
+
+
+def own_group(shape, width):
+    group = iota(shape, 0) % plane_groups(shape, width) * shape[1] + iota(shape, 1)
+    return iota(shape, 2) // width == group
+
+
+def tile_matrix(width):
+    source, target = iota((LANES, LANES), 0), iota((LANES, LANES), 1) % width
+    return jnp.where((source == 2 * target) | (source == 2 * target + 1), 0.125, 0.0)
+
+
+def gather_matrix(width, start):
+    source, target = iota((LANES, LANES), 0) % width, iota((LANES, LANES), 1) - start
+    return jnp.where(source == target, 1.0, 0.0)
 
 
 def kernel(sizes, block, b_ref, x_ref, sol_ref, res_ref, *rest):
@@ -56,8 +75,9 @@
     me = (at[0] * ny + at[1]) * nz + at[2]
     dims = [tuple(d >> l for d in block) for l in range(LEVELS)]
 
-    def place(index):
-        return (index // (ny * nz), index // nz % ny, index % nz)
+    def others():
+        moved = [[lax.rem(at[d] + k, sizes[d]) if k else at[d] for k in range(sizes[d])] for d in range(3)]
+        return [(a, b, c) for a in moved[0] for b in moved[1] for c in moved[2]][1:]
 
     xr[...] = jnp.zeros_like(xr)
     yr[...] = jnp.zeros_like(yr)
@@ -65,12 +85,8 @@
 
     barrier = pltpu.get_barrier_semaphore()
 
-    def greet(k, _):
-        pl.semaphore_signal(barrier, inc=1, device_id=place((me + k) % n), device_id_type=MESH)
-        return 0
-
-    lax.fori_loop(1, n, greet, 0)
-    pl.semaphore_wait(barrier, n - 1)
+    for target in others():
+        pl.semaphore_signal(barrier, inc=1, device_id=target, device_id_type=MESH)
 
     row_off, lane_off = [0], [0]
     for l in range(HALOED):
@@ -95,7 +111,7 @@
                 out.append((copy, upper if side else lower, lower if side else upper))
         return out
 
-    def send(r, fields, levels):
+    def send(r, fields, levels, before=lambda: None):
         for l in range(levels):
             X, Y, Z = dims[l]
             u = fields[l]
@@ -109,6 +125,7 @@
             packed = jnp.where(lane == plane, body[:, :, Z - 1:Z], jnp.where(lane == plane + X, body[:, :, 0:1], 0.0))
             packed = jnp.sum(packed, axis=0)
             zs[r, 0:Y, :] = packed if l == 0 else zs[r, 0:Y, :] + packed
+        before()
         for copy, cond, _ in halo_copies(r, levels):
             pl.when(cond)(copy.start)
 
@@ -161,23 +178,21 @@
         X, Y, _ = field.shape
         return jnp.broadcast_to(field[:, None], (X, 2, Y, LANES)).reshape(2 * X, Y, LANES)
 
-    def all_copy(k, src, dst, s_sem, r_sem):
-        return pltpu.make_async_remote_copy(
-            src_ref=src, dst_ref=dst.at[me], send_sem=s_sem.at[k], recv_sem=r_sem.at[k],
-            device_id=place((me + k) % n), device_id_type=MESH,
-        )
-
-    def to_all(step, src, dst, s_sem, r_sem, what):
-        def one(k, _):
-            copy = all_copy(k, src.at[step], dst.at[step], s_sem.at[step], r_sem.at[step])
-            getattr(copy, what)()
-            return 0
-        lax.fori_loop(1, n, one, 0)
+    def to_all(step, src, dst, s_sem, r_sem):
+        for target in others():
+            pltpu.make_async_remote_copy(
+                src_ref=src.at[step], dst_ref=dst.at[step, me], send_sem=s_sem.at[step], recv_sem=r_sem.at[step],
+                device_id=target, device_id_type=MESH,
+            ).start()
+
+    def all_done(step, dst, sem):
+        part = dst.at[step, pl.ds(0, n - 1)]
+        pltpu.make_async_copy(part, part, sem.at[step]).wait()
 
     X, Y, Z = dims[0]
     u0a[1:X + 1, TOP:TOP + Y, :] = x_ref[...]
     sol_ref[...] = x_ref[...]
-    send(0, [u0a], 1)
+    send(0, [u0a], 1, lambda: pl.semaphore_wait(barrier, n - 1))
     receive(0, [u0a], 1)
     for x0, c in chunks(0):
         mid, total = beside(0, u0a, 0, x0, c)
@@ -201,10 +216,13 @@
         for l in range(HALOED - 1):
             gref[l + 1][...] = lanes_dot(fold_xy(gref[l][...]), halve_matrix(dims[l + 1][2], 0))
         width = dims[HALOED][2]
-        own = lanes_dot(fold_xy(gref[HALOED - 1][...]), halve_matrix(width, at[2] * width))
+        own = lanes_dot(fold_xy(gref[HALOED - 1][...]), tile_matrix(width))
+        own = jnp.where(own_group(own.shape, width), own, 0.0)
+        own = jnp.sum(own.reshape(-1, plane_groups(own.shape, width), *own.shape[1:]), axis=1)
+        own = jnp.sum(own, axis=1, keepdims=True)
         gs[step] = own
         gr[step, me] = own
-        to_all(step, gs, gr, gsend, grecv, "start")
+        to_all(step, gs, gr, gsend, grecv)
         for l in range(HALOED):
             us[l][0][1:dims[l][0] + 1, TOP:TOP + dims[l][1], :] = gref[l][...]
         for sweep in range(SWEEPS - 1):
@@ -213,17 +231,22 @@
             later = [us[l][(sweep + 1) % 2] for l in range(HALOED)]
             send(r, fields, HALOED)
             if sweep == SWEEPS - 2:
-                to_all(step, gs, gr, gsend, grecv, "wait_recv")
-                rows = []
-                for i in range(nx):
-                    columns = []
-                    for j in range(ny):
-                        part = gr[step, (i * ny + j) * nz]
-                        for k in range(1, nz):
-                            part = part + gr[step, (i * ny + j) * nz + k]
-                        columns.append(part)
-                    rows.append(jnp.concatenate(columns, axis=1))
-                chain = [jnp.concatenate(rows, axis=0)]
+                all_done(step, gr, grecv)
+                cx, cy, _ = dims[HALOED]
+                per = plane_groups((cx, cy), width)
+                fine = None
+                for k in range(nz):
+                    rows = []
+                    for i in range(nx):
+                        columns = []
+                        for j in range(ny):
+                            part = gr[step, (i * ny + j) * nz + k][:, None]
+                            part = jnp.broadcast_to(part, (cx // per, per, cy, LANES)).reshape(cx, cy, LANES)
+                            columns.append(jnp.where(own_group((cx, cy, LANES), width), part, 0.0))
+                        rows.append(jnp.concatenate(columns, axis=1))
+                    spot = lanes_dot(jnp.concatenate(rows, axis=0), gather_matrix(width, k * width))
+                    fine = spot if fine is None else fine + spot
+                chain = [fine]
                 widths = [width * nz]
                 for l in range(HALOED + 1, LEVELS):
                     widths.append(widths[-1] // 2)
@@ -270,8 +293,8 @@
         sums = jnp.concatenate([jnp.sum(rz, axis=0, keepdims=True), jnp.sum(zw, axis=0, keepdims=True)], axis=0)
         ds[step] = sums
         dr[step, me] = sums
-        to_all(step, ds, dr, dsend, drecv, "start")
-        to_all(step, ds, dr, dsend, drecv, "wait_recv")
+        to_all(step, ds, dr, dsend, drecv)
+        all_done(step, dr, drecv)
         both = jnp.sum(dr[step], axis=0)
         both = jnp.sum(both, axis=1, keepdims=True)
         alpha = (both[0:1] / both[1:2])[None]
@@ -284,8 +307,8 @@
                 g0[x0:x0 + c] = renewed
 
     for step in range(STEPS):
-        to_all(step, gs, gr, gsend, grecv, "wait_send")
-        to_all(step, ds, dr, dsend, drecv, "wait_send")
+        all_done(step, gr, gsend)
+        all_done(step, dr, dsend)
     for r in range(ROUNDS):
         for copy, cond, _ in halo_copies(r, 1 if r % SWEEPS == 0 else HALOED):
             pl.when(cond)(copy.wait_send)
@@ -302,17 +325,18 @@
         f32 = jnp.float32
         vm = lambda *s: pltpu.VMEM(s, f32)
         padded = [vm(dims[l][0] + 2, dims[l][1] + 2 * TOP, LANES) for l in range(HALOED) for _ in range(2)]
-        cx, cy, _ = dims[HALOED]
+        cx, cy, width = dims[HALOED]
+        packed = cx // plane_groups((cx, cy), width)
         scratch = padded + [vm(dims[l][0], dims[l][1], LANES) for l in range(HALOED)] + [
             vm(cx * sizes[0], cy * sizes[1], LANES),
             vm(X // 2, Y, LANES), vm(X // 2, Y, LANES),
             vm(ROUNDS, 2, rows, LANES), vm(ROUNDS, 2, rows, LANES),
             vm(ROUNDS, 2, rows, 1, LANES), vm(ROUNDS, 2, rows, 1, LANES),
             vm(ROUNDS, Y, LANES), vm(ROUNDS, 2, Y, LANES),
-            vm(STEPS, cx, cy, LANES), vm(STEPS, n, cx, cy, LANES),
+            vm(STEPS, packed, 1, LANES), vm(STEPS, n, packed, 1, LANES),
             vm(STEPS, 2, LANES), vm(STEPS, n, 2, LANES),
             pltpu.SemaphoreType.DMA((ROUNDS, 6)), pltpu.SemaphoreType.DMA((ROUNDS, 6)),
-        ] + [pltpu.SemaphoreType.DMA((STEPS, n))] * 4
+        ] + [pltpu.SemaphoreType.DMA((STEPS,))] * 4
         out = jax.ShapeDtypeStruct(block, f32)
         return tuple(pl.pallas_call(
             functools.partial(kernel, sizes, block),

time: 80.1 us -> 67.5 us (0.84)
  Pallas kernels: 76.6 us -> 64 us
    pallas_call x1, Pallas kernels: 76.6 us -> 64 us  [run(): pl.pallas_call(functools.partial(kernel, sizes, block), out_shape=(out, o...]
where the time goes in v2:
time: 67.5 us; the launch traced here: 67.4 us
  Pallas kernels  64 us (95%)
  local copies, waits for them, and re-layouts  2.72 us (4%)
    pallas_call x1, Pallas kernels, run(): pl.pallas_call(functools.partial(kernel, sizes, block), out_shape=(out, o...  64 us
    unnamed x4, local copies, waits for them, and re-layouts  2.72 us

profile of v2, /device:TPU:0, one launch (start us, length us, event | category | flops | bytes accessed | tf_op | source)
XLA Modules:
  0.0 67.4 jit_solution(18320713158061684260)
XLA Ops:
  0.6 64.0 %shard_map.41 = (f32[32,32,128]{2,1,0:T(8,128)}, f32[32,32,128]{2,1,0:T(8,128)}) custom-call(f32[32,32,128]{2,1,0:T(8,128)} %b_ref.1, f32[32,32,128]{2,1,0:T(8,128)} %x_ref.1), custom_call_target="tpu_custom_call" | custom-call | tf_op jit(solution)/shard_map/pallas_call | solution.py:341
  64.6 0.0 copy-start
  64.6 1.9 %copy.6 = f32[32,32,128]{2,1,0:T(8,128)} copy(f32[32,32,128]{2,1,0:T(8,128)} %get-tuple-element.4) | data formatting | bytes 1048576
  66.6 0.0 copy-done
  66.6 0.8 %copy.7 = f32[32,32,128]{2,1,0:T(8,128)} copy(f32[32,32,128]{2,1,0:T(8,128)S(1)} %copy-done) | data formatting | bytes 1048576
Async XLA Ops:
  64.6 1.9 %copy-start = (f32[32,32,128]{2,1,0:T(8,128)S(1)}, f32[32,32,128]{2,1,0:T(8,128)}, u32[]{:S(2)}) copy-start(f32[32,32,128]{2,1,0:T(8,128)} %get-tuple-element.5) | copy-start | bytes 1572868

commit v3 on v2

--- a/solution.py
+++ b/solution.py
@@ -157,7 +157,7 @@
         return mid, total
 
     def chunks(l):
-        c = min(dims[l][0], 4)
+        c = min(dims[l][0], 8)
         return [(x0, c) for x0 in range(0, dims[l][0], c)]
 
     def inside(l, x0, c):

time: 67.5 us -> 65.8 us (0.975)
  Pallas kernels: 64 us -> 62.2 us
    pallas_call x1, Pallas kernels: 64 us -> 62.2 us  [run(): pl.pallas_call(functools.partial(kernel, sizes, block), out_shape=(out, o...]
where the time goes in v3:
time: 65.8 us; the launch traced here: 65.6 us
  Pallas kernels  62.2 us (95%)
  local copies, waits for them, and re-layouts  2.72 us (4%)
    pallas_call x1, Pallas kernels, run(): pl.pallas_call(functools.partial(kernel, sizes, block), out_shape=(out, o...  62.2 us
    unnamed x4, local copies, waits for them, and re-layouts  2.72 us

profile of v3, /device:TPU:0, one launch (start us, length us, event | category | flops | bytes accessed | tf_op | source)
XLA Modules:
  0.0 65.6 jit_solution(8860012439118518115)
XLA Ops:
  0.6 62.2 %shard_map.41 = (f32[32,32,128]{2,1,0:T(8,128)}, f32[32,32,128]{2,1,0:T(8,128)}) custom-call(f32[32,32,128]{2,1,0:T(8,128)} %b_ref.1, f32[32,32,128]{2,1,0:T(8,128)} %x_ref.1), custom_call_target="tpu_custom_call" | custom-call | tf_op jit(solution)/shard_map/pallas_call | solution.py:341
  62.9 0.0 copy-start
  62.9 1.9 %copy.6 = f32[32,32,128]{2,1,0:T(8,128)} copy(f32[32,32,128]{2,1,0:T(8,128)} %get-tuple-element.4) | data formatting | bytes 1048576
  64.8 0.0 copy-done
  64.8 0.8 %copy.7 = f32[32,32,128]{2,1,0:T(8,128)} copy(f32[32,32,128]{2,1,0:T(8,128)S(1)} %copy-done) | data formatting | bytes 1048576
Async XLA Ops:
  62.9 1.9 %copy-start = (f32[32,32,128]{2,1,0:T(8,128)S(1)}, f32[32,32,128]{2,1,0:T(8,128)}, u32[]{:S(2)}) copy-start(f32[32,32,128]{2,1,0:T(8,128)} %get-tuple-element.5) | copy-start | bytes 1572868
